TPU v7x, 32 devices: a 4x4x1 block of a 4x4x8 slice. The times are simulated.
32 devices in a mesh: replica: 1 (over z), heads: 4 (over y), model: 8 (over x, core).
Axes of the slice: x: 4, y: 4, z: 1, core: 2. Of those that a mesh axis runs over, the one named last changes fastest.
The devices are a block of a 4x4x8 slice.
Arguments:
- tokens: bfloat16 [256, 4096], P('replica')
- w_query: bfloat16 [4096, 4096], P(None, ('heads', 'model'))
- w_key: bfloat16 [4096, 1024], replicated
- w_value: bfloat16 [4096, 1024], replicated
- w_out: bfloat16 [4096, 4096], P(('heads', 'model'))
- key_cache: bfloat16 [256, 8, 1024, 128], P(('replica', 'model'))
- value_cache: bfloat16 [256, 8, 1024, 128], P(('replica', 'model'))
- lengths: int32 [256], P(('replica', 'model'))
Outputs:
- output 1: bfloat16 [256, 4096], P('replica')
- output 2: bfloat16 [256, 8, 128], P(('replica', 'model'))
- output 3: bfloat16 [256, 8, 128], P(('replica', 'model'))
All inputs are finite; a program needn't handle non-finite values.
Results may differ from a plain program's by a relative error of at most 0.00217124.
Values are sent between devices in bfloat16 or wider.
A program may use at most 768 MiB of HBM per device.

v0:
```python
import jax
import jax.numpy as jnp
from jax import lax
from jax.sharding import PartitionSpec as P


def attend(queries, key_rows, value_rows, key_last, value_last, seq_len):
    score_scale = queries.shape[-1] ** -0.5
    scores = jnp.einsum("bgrd,bgtd->bgrt", queries, key_rows, preferred_element_type=jnp.float32) * score_scale
    score_new = jnp.einsum("bgrd,bgd->bgr", queries, key_last, preferred_element_type=jnp.float32) * score_scale
    positions = lax.broadcasted_iota(jnp.int32, (1, 1, 1, key_rows.shape[2]), 3)
    scores = jnp.where(positions < seq_len[:, None, None, None], scores, -jnp.inf)
    score_max = jnp.maximum(jnp.max(scores, axis=-1), score_new)
    weights = jnp.exp(scores - score_max[..., None])
    weight_new = jnp.exp(score_new - score_max)
    denom_sum = jnp.sum(weights, axis=-1) + weight_new
    weighted_sum = jnp.einsum("bgrt,bgtd->bgrd", weights.astype(jnp.bfloat16), value_rows, preferred_element_type=jnp.float32)
    weighted_sum = weighted_sum + weight_new.astype(jnp.bfloat16).astype(jnp.float32)[..., None] * value_last.astype(jnp.float32)[:, :, None, :]
    return (weighted_sum / denom_sum[..., None]).astype(jnp.bfloat16)


def solution(mesh):
    heads_count = mesh.shape["heads"]
    model_count = mesh.shape["model"]

    def local_step(tokens, w_query, w_key, w_value, w_out, key_cache, value_cache, lengths):
        batch_all = tokens.shape[0]
        local_rows = key_cache.shape[0]
        kv_count = key_cache.shape[1]
        head_dim = key_cache.shape[3]
        heads_local = w_query.shape[1] // head_dim
        heads_shard = heads_local * model_count
        group_size = heads_shard * heads_count // kv_count
        shard_groups = max(1, heads_shard // group_size)
        head_index = lax.axis_index("heads")
        model_index = lax.axis_index("model")
        queries = jnp.dot(tokens, w_query, preferred_element_type=jnp.float32).astype(jnp.bfloat16)
        queries = lax.all_to_all(queries.reshape(batch_all, heads_local, head_dim), "model", 0, 1, tiled=True)
        own_tokens = lax.dynamic_slice_in_dim(tokens, model_index * local_rows, local_rows, 0)
        key_new = jnp.dot(own_tokens, w_key, preferred_element_type=jnp.float32).astype(jnp.bfloat16)
        key_new = key_new.reshape(local_rows, kv_count, head_dim)
        value_new = jnp.dot(own_tokens, w_value, preferred_element_type=jnp.float32).astype(jnp.bfloat16)
        value_new = value_new.reshape(local_rows, kv_count, head_dim)
        first_group = head_index * heads_shard // group_size
        attended = attend(
            queries.reshape(local_rows, shard_groups, heads_shard // shard_groups, head_dim),
            lax.dynamic_slice_in_dim(key_cache, first_group, shard_groups, 1),
            lax.dynamic_slice_in_dim(value_cache, first_group, shard_groups, 1),
            lax.dynamic_slice_in_dim(key_new, first_group, shard_groups, 1),
            lax.dynamic_slice_in_dim(value_new, first_group, shard_groups, 1),
            lengths,
        )
        attended = lax.all_to_all(attended.reshape(local_rows, heads_shard, head_dim), "model", 1, 0, tiled=True)
        partial = jnp.dot(attended.reshape(batch_all, heads_local * head_dim), w_out, preferred_element_type=jnp.float32)
        mixed_sum = lax.psum(partial, ("heads", "model"))
        out_tokens = (tokens.astype(jnp.float32) + mixed_sum).astype(jnp.bfloat16)
        return (out_tokens, key_new, value_new)

    cache_spec = P(("replica", "model"), None, None, None)
    new_spec = P(("replica", "model"), None, None)
    return jax.shard_map(
        local_step,
        mesh=mesh,
        in_specs=(P("replica", None), P(None, ("heads", "model")), P(None, None), P(None, None), P(("heads", "model"), None), cache_spec, cache_spec, P(("replica", "model"))),
        out_specs=(P("replica", None), new_spec, new_spec),
        check_vma=False,
    )
```

profile of v0, /device:TPU:97, one launch (start us, length us, event | category | flops | bytes accessed | tf_op | source)
XLA Modules:
  0.0 173.6 jit_solution(3483958859663637422)
XLA Ops:
  7.2 0.0 copy-start
  7.2 0.0 copy-start.1
  7.2 2.7 %fusion.12 = bf16[256,1,128]{2,0,1:T(8,128)(2,1)S(1)} fusion(bf16[256,4096]{1,0:T(8,128)(2,1)} %param.8, bf16[4096,128]{1,0:T(8,128)(2,1)} %param.9), kind=kOutput, calls=%fused_computation.12 | convolution fusion | flops 268468224 | bytes 3211264 | tf_op jit(solution)/shard_map/dot_general | solution.py:37
  9.9 0.5 broadcast.18
  10.4 0.7 reduce
  11.1 0.6 reshape.59
  11.7 6.0 %all-to-all-start = ((bf16[8,2,2048]{2,1,0:T(2,128)(2,1)}), bf16[8,2,2048]{2,1,0:T(2,128)(2,1)S(1)}, u32[]{:S(2)}, u32[]{:S(2)}) async-start(bf16[8,2,2048]{2,1,0:T(2,128)(2,1)} %reshape.59), calls=%async_computation | async-start | bytes 131072 | tf_op jit(solution)/shard_map/all_to_all | solution.py:38
  17.8 0.0 all-reduce.2.cloned.1.call-start
  17.8 0.7 iota_compare_fusion
  18.5 0.0 copy-start.2
  18.5 5.2 %fusion.10 = bf16[4,8,8,128]{3,1,2,0:T(8,128)(2,1)S(1)} fusion(bf16[4096,1024]{1,0:T(8,128)(2,1)} %param.10, bf16[256,4096]{1,0:T(8,128)(2,1)} %param.8, s32[]{:T(128)S(6)} %select_n.21), kind=kOutput, calls=%fused_computation.10 | convolution fusion | flops 268468224 | bytes 8716292 | tf_op jit(solution)/shard_map/dot_general | solution.py:40
  23.7 0.0 copy-done.1
  23.7 0.6 copy-done.2
  24.4 0.0 copy-start.3
  24.4 1.6 fusion.11
  25.9 0.0 copy-start.4
  26.0 0.0 all-to-all-done
  26.0 0.1 reshape.60
  26.2 0.2 fusion.28
  26.4 11.2 %fusion.35 = (f32[32,2,4]{2,1,0:T(2,128)S(1)}, f32[32,2,4,1024]{3,2,1,0:T(4,128)}) fusion(bf16[32,2,4,128]{3,2,1,0:T(4,128)(2,1)S(1)} %bitcast.31, bf16[32,8,1024,128]{3,2,1,0:T(8,128)(2,1)} %param.13, s32[]{:T(128)S(6)} %select_n.19, pred[32,1024]{1,0:T(8,128)(4,1)S(1)} %iota_compare_fusion), kind=kOutput, calls=%fused_computation.35 | convolution fusion | flops 67895040 | bytes 17925124 | tf_op jit(solution)/shard_map/bgrd,bgtd->bgrt/dot_general | solution.py:9
  37.6 0.0 copy-done.3
  37.6 0.0 copy-done.4
  37.6 1.8 %fusion.22 = f32[32,2,4]{2,1,0:T(2,128)S(1)} fusion(f32[32,2,4,1024]{3,2,1,0:T(4,128)} %get-tuple-element.6, f32[32,2,4]{2,1,0:T(2,128)S(1)} %multiply_maximum_fusion), kind=kLoop, calls=%fused_computation.17 | loop fusion | flops 524032 | bytes 1050624 | tf_op jit(solution)/shard_map/reduce_sum | solution.py:16
  39.4 8.6 %fusion.19 = bf16[32,2,4,128]{3,2,1,0:T(4,128)(2,1)S(1)} fusion(bf16[32,8,1024,128]{3,2,1,0:T(8,128)(2,1)} %param.14, s32[]{:T(128)S(6)} %select_n.19, f32[32,2,4,1024]{3,2,1,0:T(4,128)} %get-tuple-element.6, f32[32,2,4]{2,1,0:T(2,128)S(1)} %multiply_maximum_fusion, f32[32,2,4]{2,1,0:T(2,128)S(1)} %get-tuple-element.4, ...), kind=kOutput, calls=%fused_computation.16 | convolution fusion | flops 67764224 | bytes 17927172 | tf_op jit(solution)/shard_map/bgrt,bgtd->bgrd/dot_general | solution.py:17
  48.0 9.5 %all_to_all.30 = bf16[32,8,128]{2,0,1:T(8,128)(2,1)S(1)} all-to-all(bf16[32,8,128]{2,0,1:T(8,128)(2,1)S(1)} %copy.19), channel_id=1, replica_groups=mesh['replica'=1,'heads'=4,'model'=8] {'model'}, dimensions={1} | all-to-all | bytes 131072 | tf_op jit(solution)/shard_map/all_to_all | solution.py:53
  57.5 0.0 copy-done
  57.5 2.7 %fusion.36 = f32[256,4096]{1,0:T(8,128)} fusion(bf16[256,128]{1,0:T(8,128)(2,1)S(1)} %bitcast.33, bf16[128,4096]{1,0:T(8,128)(2,1)S(1)} %copy-done), kind=kOutput, calls=%fused_computation.36 | convolution fusion | flops 268435456 | bytes 5308416 | tf_op jit(solution)/shard_map/dot_general | solution.py:54
  60.2 0.1 all-reduce.2.cloned.1.call-update
  60.2 102.5 %all-reduce.2.cloned.1.call-done = f32[256,4096]{1,0:T(8,128)} async-done(((f32[256,4096]{1,0:T(8,128)}), f32[256,4096]{1,0:T(8,128)}) %all-reduce.2.cloned.1.call-update) | async-done | bytes 4194320 | tf_op jit(solution)/shard_map/psum | solution.py:55
  162.7 4.1 %add_convert_fusion = bf16[256,4096]{1,0:T(8,128)(2,1)} fusion(f32[256,4096]{1,0:T(8,128)} %all-reduce.2.cloned.1.call-done, bf16[256,4096]{1,0:T(8,128)(2,1)S(1)} %copy-done.1), kind=kLoop, calls=%fused_computation.4 | loop fusion | flops 3145728 | bytes 8388608 | tf_op jit(solution)/shard_map/convert_element_type | solution.py:56
  (9 shorter events, 0.2 us)
Async XLA Ops:
  7.2 50.3 %copy-start = (bf16[128,4096]{1,0:T(8,128)(2,1)S(1)}, bf16[128,4096]{1,0:T(8,128)(2,1)}, u32[]{:S(2)}) copy-start(bf16[128,4096]{1,0:T(8,128)(2,1)} %param.12) | copy-start | bytes 3145732
  7.2 16.5 %copy-start.1 = (bf16[256,4096]{1,0:T(8,128)(2,1)S(1)}, bf16[256,4096]{1,0:T(8,128)(2,1)}, u32[]{:S(2)}) copy-start(bf16[256,4096]{1,0:T(8,128)(2,1)} %param.8) | copy-start | bytes 6291460
  11.7 14.3 %all-to-all-start = ((bf16[8,2,2048]{2,1,0:T(2,128)(2,1)}), bf16[8,2,2048]{2,1,0:T(2,128)(2,1)S(1)}, u32[]{:S(2)}, u32[]{:S(2)}) async-start(bf16[8,2,2048]{2,1,0:T(2,128)(2,1)} %reshape.59), calls=%async_computation | async-start | bytes 131072 | tf_op jit(solution)/shard_map/all_to_all | solution.py:38
  17.8 145.0 %all-reduce.2.cloned.1.call-start = ((), (), s32[]{:S(2)}) async-start(), calls=%async_computation.2 | async-start | bytes 8388608 | tf_op jit(solution)/shard_map/psum | solution.py:55
  18.5 5.8 %copy-start.2 = (bf16[4096,1024]{1,0:T(8,128)(2,1)S(1)}, bf16[4096,1024]{1,0:T(8,128)(2,1)}, u32[]{:S(2)}) copy-start(bf16[4096,1024]{1,0:T(8,128)(2,1)} %param.11) | copy-start | bytes 25165828
  24.4 13.2 %copy-start.3 = (bf16[4,8,8,128]{3,2,1,0:T(8,128)(2,1)}, bf16[4,8,8,128]{3,2,1,0:T(8,128)(2,1)S(1)}, u32[]{:S(2)}) copy-start(bf16[4,8,8,128]{3,2,1,0:T(8,128)(2,1)S(1)} %copy.23) | copy-start | bytes 196612
  25.9 11.6 %copy-start.4 = (bf16[4,8,8,128]{3,2,1,0:T(8,128)(2,1)}, bf16[4,8,8,128]{3,2,1,0:T(8,128)(2,1)S(1)}, u32[]{:S(2)}) copy-start(bf16[4,8,8,128]{3,2,1,0:T(8,128)(2,1)S(1)} %copy.24) | copy-start | bytes 196612
Sparse Core Ops, SparseCore 0:
  60.3 102.3 all-reduce.1
where the time goes:
time: 174 us
  waiting for transfers between devices  103 us (59%)
  matrix products  32 us (18%)
  between operations  14.2 us (8%)
  blocking collectives  9.47 us (5%)
  other arithmetic  7.32 us (4%)
  starting transfers between devices  6.02 us (3%)
  local copies, waits for them, and re-layouts  2.02 us (1%)
    psum x1, waiting for transfers between devices, local_step(): mixed_sum = lax.psum(partial, ('heads', 'model'))  102 us
    dot_general x1, matrix products, attend(): jnp.einsum('bgrd,bgtd->bgrt', queries, key_rows, preferred_element_type=j...  11.2 us
    all_to_all x1, blocking collectives, local_step(): lax.all_to_all(attended.reshape(local_rows, heads_shard, head_dim), 'mode...  9.47 us
    dot_general x1, matrix products, attend(): jnp.einsum('bgrt,bgtd->bgrd', weights.astype(jnp.bfloat16), value_rows, p...  8.55 us
    all_to_all x1, starting transfers between devices, local_step(): lax.all_to_all(queries.reshape(batch_all, heads_local, head_dim), 'model'...  6.02 us
    dot_general x1, matrix products, local_step(): jnp.dot(own_tokens, w_key, preferred_element_type=jnp.float32)  5.16 us
    convert_element_type x1, other arithmetic, local_step(): out_tokens = (tokens.astype(jnp.float32) + mixed_sum).astype(jnp.bfloat16)  4.07 us
  transfers between devices with their start and end apart: 2, of which 1 were waited for; matrix products, arithmetic and copies ran while one was open for 4% of the time, Pallas kernels for 0%

commit v1 on v0

v1 whole, which is shorter than its diff:
```python
import functools

import jax
import jax.numpy as jnp
from jax import lax
from jax.experimental import pallas as pl
from jax.experimental.pallas import tpu as pltpu
from jax.sharding import PartitionSpec as P

CORES = 2
ROW_TILE = 16
SEQ_STEP = 4
MESH = pl.DeviceIdType.MESH
F32 = jnp.float32
BF16 = jnp.bfloat16


def remote(src, dst, send_sem, recv_sem, head_pos, model_pos):
    return pltpu.make_async_remote_copy(
        src_ref=src,
        dst_ref=dst,
        send_sem=send_sem,
        recv_sem=recv_sem,
        device_id={"heads": head_pos, "model": model_pos},
        device_id_type=MESH,
    )


def step_kernel(
    dims,
    tokens, w_query, w_key, w_value, w_out, key_cache, value_cache, lengths,
    out, key_out, value_out,
    tok_v, wq_v, wkv_v, kbuf, vbuf, wo_v, q_send, q_recv, q_wide, new_v, new_wide, p_v, l_v, o_wide, o_v, out_v,
    load_sem, wkv_sem, kv_sem, own_sem, q_ss, q_rs, w_ss, w_rs, f_ss, f_rs, n_ss, n_rs, a_ss, a_rs, g_ss, g_rs, d_ss, d_rs, s_sem,
):
    H, NX = dims["heads"], dims["chips_x"]
    M = NX * CORES
    lr, T, dh, D = dims["rows"], dims["context"], dims["head_dim"], dims["width"]
    kvs, qs, gs = dims["kv_shard"], dims["q_shard"], dims["group"]
    cols = dims["cols"]
    kvw = kvs * dh
    qw = qs * dh
    n_load = dims["n_load"]
    kc = D // n_load
    h = lax.axis_index("heads")
    m = lax.axis_index("model")
    x = m // CORES
    c = m % CORES
    partner = x * CORES + (1 - c)
    chip = h * NX + x
    R = H

    tok_loads, wq_loads = [], []
    for i in range(n_load):
        a = pltpu.make_async_copy(tokens.at[:, :, :, pl.ds(i * kc, kc)], tok_v.at[:, :, :, pl.ds(i * kc, kc)], load_sem.at[2 * i])
        b = pltpu.make_async_copy(w_query.at[pl.ds(i * kc, kc), :], wq_v.at[pl.ds(i * kc, kc), :], load_sem.at[2 * i + 1])
        a.start()
        b.start()
        tok_loads.append(a)
        wq_loads.append(b)
    kv_cols = pl.ds(pl.multiple_of(h * kvw, kvw), kvw)
    wk_load = pltpu.make_async_copy(w_key.at[:, kv_cols], wkv_v.at[0], wkv_sem.at[0])
    wv_load = pltpu.make_async_copy(w_value.at[:, kv_cols], wkv_v.at[1], wkv_sem.at[1])
    wk_load.start()
    wv_load.start()
    my_cols = pl.ds(pl.multiple_of(chip * cols, cols), cols)
    own_load = pltpu.make_async_copy(w_out.at[:, my_cols], wo_v.at[h * M + m], own_sem)
    own_load.start()

    steps = lr // SEQ_STEP

    def k_load(i):
        return pltpu.make_async_copy(
            key_cache.at[pl.ds(i * SEQ_STEP, SEQ_STEP), pl.ds(h * kvs, kvs)], kbuf.at[pl.ds(i * SEQ_STEP, SEQ_STEP)], kv_sem.at[0, i])

    def v_load(i):
        return pltpu.make_async_copy(
            value_cache.at[pl.ds(i * SEQ_STEP, SEQ_STEP), pl.ds(h * kvs, kvs)], vbuf.at[pl.ds(i * SEQ_STEP, SEQ_STEP)], kv_sem.at[1, i])

    for i in range(steps):
        k_load(i).start()
        v_load(i).start()

    barrier = pltpu.get_barrier_semaphore()
    peers = 0
    for dy in range(H):
        for dx in range(NX):
            if dx or dy:
                pl.semaphore_signal(barrier, inc=1, device_id={"heads": (h + dy) % H, "model": ((x + dx) % NX) * CORES + c}, device_id_type=MESH)
                peers += 1
    for dx in range(NX):
        pl.semaphore_signal(barrier, inc=1, device_id={"heads": h, "model": ((x + dx) % NX) * CORES + (1 - c)}, device_id_type=MESH)
        peers += 1

    acc = jnp.zeros((M * lr, dh), F32)
    for i in range(n_load):
        tok_loads[i].wait()
        wq_loads[i].wait()
        t = tok_v[:, :, :, pl.ds(i * kc, kc)].reshape(M * lr, kc)
        acc = acc + jnp.dot(t, wq_v[pl.ds(i * kc, kc), :], preferred_element_type=F32)
    q_send[...] = acc.astype(BF16).reshape(M, lr, dh)

    pl.semaphore_wait(barrier, peers)

    q_copies = []
    for k in sorted(range(1, M), key=lambda k: -min(k, M - k)):
        to = (m + k) % M
        cp = remote(q_send.at[to], q_recv.at[m], q_ss.at[k], q_rs.at[k], h, to)
        cp.start()
        q_copies.append(cp)

    w_copies = []
    order = [(dx, dy) for dx in range(NX) for dy in range(H) if dx or dy]
    order.sort(key=lambda d: -(min(d[0], NX - d[0]) + min(d[1], H - d[1])))
    for dx, dy in order:
        tx, ty = (x + dx) % NX, (h + dy) % H
        to_cols = pl.ds(pl.multiple_of((ty * NX + tx) * cols, cols), cols)
        cp = remote(w_out.at[:, to_cols], wo_v.at[h * M + m], w_ss.at[dy * NX + dx], w_rs.at[dy * NX + dx], ty, tx * CORES + c)
        cp.start()
        w_copies.append(cp)

    q_recv[m] = q_send[m]

    own_tok = tok_v[x, c]
    wk_load.wait()
    key_new = jnp.dot(own_tok, wkv_v[0], preferred_element_type=F32).astype(BF16)
    wv_load.wait()
    value_new = jnp.dot(own_tok, wkv_v[1], preferred_element_type=F32).astype(BF16)
    new_v[0, :, kv_cols] = key_new
    new_v[1, :, kv_cols] = value_new
    for g in range(kvs):
        new_wide[pl.ds(g * lr, lr), :] = key_new[:, g * dh:(g + 1) * dh].astype(F32)
        new_wide[pl.ds((kvs + g) * lr, lr), :] = value_new[:, g * dh:(g + 1) * dh].astype(F32)

    def new_block(pos):
        return new_v.at[:, :, pl.ds(pl.multiple_of(pos * kvw, kvw), kvw)]

    n_copies = []
    for k in range(1, H):
        cp = remote(new_block(h), new_block(h), n_ss.at[k], n_rs.at[k], (h + k) % H, m)
        cp.start()
        n_copies.append(cp)

    for k in range(1, M):
        frm = (m + M - k) % M
        remote(q_recv.at[frm], q_recv.at[frm], q_ss.at[k], q_rs.at[k], h, m).wait_recv()
    q_wide[...] = q_recv[...].astype(F32).reshape(M * lr, dh)

    scale = dh ** -0.5
    row = lax.broadcasted_iota(jnp.int32, (qs, dh), 0)
    pos = lax.broadcasted_iota(jnp.int32, (qs, T), 1)
    tile_row = lax.broadcasted_iota(jnp.int32, (ROW_TILE, dh), 0)

    def with_new(buf, which, b):
        parts = []
        fresh = new_wide[pl.ds(which * kvs * lr + b, kvs, stride=lr), :]
        for g in range(kvs):
            tail = buf[b, g, pl.ds(T - ROW_TILE, ROW_TILE), :].astype(F32)
            tail = jnp.where(tile_row == ROW_TILE - 1, jnp.broadcast_to(fresh[g:g + 1], (ROW_TILE, dh)), tail).astype(BF16)
            parts.append(jnp.concatenate([buf[b, g, pl.ds(0, T - ROW_TILE), :], tail], axis=0))
        return jnp.concatenate(parts, axis=1)

    def scores_of(i):
        for s in range(SEQ_STEP):
            b = i * SEQ_STEP + s
            qb = q_wide[pl.ds(b, qs, stride=lr), :]
            qb = jnp.concatenate([jnp.where(row // gs == g, qb, 0.0) for g in range(kvs)], axis=1).astype(BF16)
            sc = lax.dot_general(qb, with_new(kbuf, 0, b), (((1,), (1,)), ((), ())), preferred_element_type=F32) * scale
            sc = jnp.where(jnp.logical_or(pos < lengths[b], pos == T - 1), sc, -jnp.inf)
            top = jnp.max(sc, axis=1, keepdims=True)
            p = jnp.exp(sc - top)
            l_v[i % 2, s] = jnp.broadcast_to(jnp.sum(p, axis=1, keepdims=True), (qs, dh))
            p_v[i % 2, s] = p.astype(BF16)

    def values_of(i):
        for s in range(SEQ_STEP):
            b = i * SEQ_STEP + s
            wide = jnp.dot(p_v[i % 2, s], with_new(vbuf, 1, b), preferred_element_type=F32)
            o = wide[:, :dh]
            for g in range(1, kvs):
                o = jnp.where(row // gs == g, wide[:, g * dh:(g + 1) * dh], o)
            o_wide[pl.ds(b * qs, qs), :] = o / l_v[i % 2, s]

    def peer_first(k):
        return (h + k * c) % H, ((x + k * (1 - c)) % NX) * CORES + c

    def peer_second(k):
        return (h + k * (1 - c)) % H, ((x + k * c) % NX) * CORES + c

    def source(k1, k2):
        return (h + 2 * R - k1 * c - k2 * (1 - c)) % H, (x + 2 * R - k1 * (1 - c) - k2 * c) % NX

    hops = [k for k in range(1, R)]
    hops.sort(key=lambda k: -min(k, R - k))

    def o_block(g, sy, sx):
        return o_v.at[sx, pl.ds(g * ROW_TILE, ROW_TILE), pl.ds(pl.multiple_of(sy * qw, qw), qw)]

    def a_send_own(g):
        for j in range(qs):
            o_v[x, pl.ds(g * ROW_TILE, ROW_TILE), pl.ds(pl.multiple_of(h * qw + j * dh, dh), dh)] = (
                o_wide[pl.ds(g * ROW_TILE * qs + j, ROW_TILE, stride=qs), :].astype(BF16))
        blk = o_block(g, h, x)
        for k in hops:
            remote(blk, blk, a_ss.at[g, k * R], a_rs.at[g, k * R], *peer_first(k)).start()
        for k in hops:
            remote(blk, blk, a_ss.at[g, k], a_rs.at[g, k], *peer_second(k)).start()

    def a_forward(g):
        for k1 in (*hops[1:], hops[0]):
            blk = o_block(g, *source(k1, 0))
            remote(blk, blk, a_ss.at[g, k1 * R], a_rs.at[g, k1 * R], h, m).wait_recv()
            for k2 in hops:
                remote(blk, blk, a_ss.at[g, k1 * R + k2], a_rs.at[g, k1 * R + k2], *peer_second(k2)).start()

    groups = lr // ROW_TILE
    per_group = ROW_TILE // SEQ_STEP

    k_load(0).wait()
    scores_of(0)

    def body(i, carry):
        for g in range(groups - 1):
            @pl.when(i == (g + 1) * per_group + 1)
            def _():
                a_send_own(g)
        k_load(i).wait()
        v_load(i - 1).wait()
        scores_of(i)
        values_of(i - 1)
        return carry

    lax.fori_loop(1, steps, body, 0)
    v_load(steps - 1).wait()
    values_of(steps - 1)
    a_send_own(groups - 1)
    for g in range(groups - 1):
        a_forward(g)

    own_load.wait()
    def wo_forward(sy, sx, idx):
        blk = wo_v.at[sy * M + sx * CORES + c]
        remote(blk, blk, f_ss.at[idx], f_rs.at[idx], h, partner).start()

    wo_forward(h, x, 0)
    a_forward(groups - 1)
    for dx, dy in order:
        sx, sy = (x + NX - dx) % NX, (h + H - dy) % H
        blk = wo_v.at[sy * M + sx * CORES + c]
        remote(blk, blk, w_ss.at[dy * NX + dx], w_rs.at[dy * NX + dx], h, m).wait_recv()
        wo_forward(sy, sx, dy * NX + dx)

    def new_store(which, dst):
        return pltpu.make_async_copy(new_v.at[which], dst, s_sem.at[which])

    for k in range(1, H):
        blk = new_block((h + H - k) % H)
        remote(blk, blk, n_ss.at[k], n_rs.at[k], h, m).wait_recv()
    new_store(0, key_out).start()
    new_store(1, value_out).start()

    for dx, dy in [(0, 0)] + order:
        sx, sy = (x + NX - dx) % NX, (h + H - dy) % H
        blk = wo_v.at[sy * M + sx * CORES + (1 - c)]
        remote(blk, blk, f_ss.at[dy * NX + dx], f_rs.at[dy * NX + dx], h, m).wait_recv()
    for g in range(groups):
        for k1 in range(R):
            for k2 in range(1, R):
                blk = o_block(g, *source(k1, k2))
                remote(blk, blk, a_ss.at[g, k1 * R + k2], a_rs.at[g, k1 * R + k2], h, m).wait_recv()

    mixed = jnp.dot(o_v[...].reshape(NX * lr, H * qw), wo_v[...].reshape(H * M * dh, cols), preferred_element_type=F32)
    mixed = tok_v[:, c, :, my_cols].astype(F32) + mixed.reshape(NX, lr, cols)
    out_v[:, c, :, my_cols] = mixed.astype(BF16)

    def out_block(core, sy, sx):
        return out_v.at[:, core, :, pl.ds(pl.multiple_of((sy * NX + sx) * cols, cols), cols)]

    def d_forward(k1, k2):
        blk = out_block(c, *source(k1, k2))
        remote(blk, blk, d_ss.at[k1 * R + k2], d_rs.at[k1 * R + k2], h, partner).start()

    blk = out_block(c, h, x)
    for k in hops:
        remote(blk, blk, g_ss.at[k * R], g_rs.at[k * R], *peer_first(k)).start()
    for k in hops:
        remote(blk, blk, g_ss.at[k], g_rs.at[k], *peer_second(k)).start()
    d_forward(0, 0)
    for k1 in (*hops[1:], hops[0]):
        blk = out_block(c, *source(k1, 0))
        remote(blk, blk, g_ss.at[k1 * R], g_rs.at[k1 * R], h, m).wait_recv()
        for k2 in hops:
            remote(blk, blk, g_ss.at[k1 * R + k2], g_rs.at[k1 * R + k2], *peer_second(k2)).start()
        d_forward(k1, 0)
    for k1 in range(R):
        for k2 in range(1, R):
            blk = out_block(c, *source(k1, k2))
            remote(blk, blk, g_ss.at[k1 * R + k2], g_rs.at[k1 * R + k2], h, m).wait_recv()
            d_forward(k1, k2)
    own_store = pltpu.make_async_copy(out_v.at[:, c], out.at[:, c], s_sem.at[2])
    own_store.start()
    for k1 in range(R):
        for k2 in range(R):
            sy, sx = (h + 2 * R - k1 * (1 - c) - k2 * c) % H, (x + 2 * R - k1 * c - k2 * (1 - c)) % NX
            blk = out_block(1 - c, sy, sx)
            remote(blk, blk, d_ss.at[k1 * R + k2], d_rs.at[k1 * R + k2], h, m).wait_recv()
    other_store = pltpu.make_async_copy(out_v.at[:, 1 - c], out.at[:, 1 - c], s_sem.at[3])
    other_store.start()

    for cp in q_copies + w_copies + n_copies:
        cp.wait_send()
    for idx in range(H * NX):
        blk = wo_v.at[0]
        remote(blk, blk, f_ss.at[idx], f_rs.at[idx], h, m).wait_send()
    for g in range(groups):
        for idx in range(1, R * R):
            blk = o_block(g, h, x)
            remote(blk, blk, a_ss.at[g, idx], a_rs.at[g, idx], h, m).wait_send()
    for idx in range(R * R):
        blk = out_block(c, h, x)
        if idx:
            remote(blk, blk, g_ss.at[idx], g_rs.at[idx], h, m).wait_send()
        remote(blk, blk, d_ss.at[idx], d_rs.at[idx], h, m).wait_send()
    new_store(0, key_out).wait()
    new_store(1, value_out).wait()
    own_store.wait()
    other_store.wait()


def solution(mesh):
    heads_count = mesh.shape["heads"]
    model_count = mesh.shape["model"]

    def local_step(tokens, w_query, w_key, w_value, w_out, key_cache, value_cache, lengths):
        batch_all, width = tokens.shape
        rows, kv_count, context, head_dim = key_cache.shape
        chips_x = model_count // CORES
        q_shard = model_count * (w_query.shape[1] // head_dim)
        group = q_shard * heads_count // kv_count
        kv_shard = q_shard // group
        cols = width // (heads_count * chips_x)
        dims = dict(heads=heads_count, chips_x=chips_x, rows=rows, context=context, head_dim=head_dim, width=width,
                    kv_shard=kv_shard, q_shard=q_shard, group=group, cols=cols, n_load=4)
        assert heads_count == chips_x and q_shard == model_count
        steps = rows // SEQ_STEP
        groups = rows // ROW_TILE
        ring = heads_count
        any_spec = pl.BlockSpec(memory_space=pl.ANY)
        dma = pltpu.SemaphoreType.DMA
        out, key_new, value_new = pl.pallas_call(
            functools.partial(step_kernel, dims),
            out_shape=(
                jax.ShapeDtypeStruct((chips_x, CORES, rows, width), BF16),
                jax.ShapeDtypeStruct((rows, kv_count * head_dim), BF16),
                jax.ShapeDtypeStruct((rows, kv_count * head_dim), BF16),
            ),
            in_specs=[any_spec] * 7 + [pl.BlockSpec(memory_space=pltpu.SMEM)],
            out_specs=(any_spec,) * 3,
            scratch_shapes=[
                pltpu.VMEM((chips_x, CORES, rows, width), BF16),
                pltpu.VMEM((width, head_dim), BF16),
                pltpu.VMEM((2, width, kv_shard * head_dim), BF16),
                pltpu.VMEM((rows, kv_shard, context, head_dim), BF16),
                pltpu.VMEM((rows, kv_shard, context, head_dim), BF16),
                pltpu.VMEM((heads_count * model_count, head_dim, cols), BF16),
                pltpu.VMEM((model_count, rows, head_dim), BF16),
                pltpu.VMEM((model_count, rows, head_dim), BF16),
                pltpu.VMEM((model_count * rows, head_dim), F32),
                pltpu.VMEM((2, rows, kv_count * head_dim), BF16),
                pltpu.VMEM((2 * kv_shard * rows, head_dim), F32),
                pltpu.VMEM((2, SEQ_STEP, q_shard, context), BF16),
                pltpu.VMEM((2, SEQ_STEP, q_shard, head_dim), F32),
                pltpu.VMEM((rows * q_shard, head_dim), F32),
                pltpu.VMEM((chips_x, rows, heads_count * q_shard * head_dim), BF16),
                pltpu.VMEM((chips_x, CORES, rows, width), BF16),
                dma((8,)),
                dma((2,)),
                dma((2, steps)),
                dma,
                dma((model_count,)),
                dma((model_count,)),
                dma((ring * ring,)),
                dma((ring * ring,)),
                dma((ring * ring,)),
                dma((ring * ring,)),
                dma((ring,)),
                dma((ring,)),
                dma((groups, ring * ring)),
                dma((groups, ring * ring)),
                dma((ring * ring,)),
                dma((ring * ring,)),
                dma((ring * ring,)),
                dma((ring * ring,)),
                dma((4,)),
            ],
            compiler_params=pltpu.CompilerParams(
                collective_id=0, has_side_effects=True, vmem_limit_bytes=60 * 1024 * 1024
            ),
            name="decode_step",
        )(
            tokens.reshape(chips_x, CORES, rows, width), w_query, w_key, w_value, w_out, key_cache, value_cache, lengths
        )
        new_shape = (rows, kv_count, head_dim)
        return out.reshape(batch_all, width), key_new.reshape(new_shape), value_new.reshape(new_shape)

    cache_spec = P(("replica", "model"), None, None, None)
    new_spec = P(("replica", "model"), None, None)
    return jax.shard_map(
        local_step,
        mesh=mesh,
        in_specs=(P("replica", None), P(None, ("heads", "model")), P(None, None), P(None, None), P(("heads", "model"), None), cache_spec, cache_spec, P(("replica", "model"))),
        out_specs=(P("replica", None), new_spec, new_spec),
        check_vma=False,
    )
```

time: 174 us -> 67 us (0.39)
  waiting for transfers between devices: 103 us -> 0 us
  Pallas kernels: 0 us -> 60.1 us
  matrix products: 32 us -> 0 us
  between operations: 14.2 us -> 0.64 us
  blocking collectives: 9.47 us -> 0 us
  other arithmetic: 7.32 us -> 0 us
  starting transfers between devices: 6.02 us -> 0 us
  local copies, waits for them, and re-layouts: 2.02 us -> 6.09 us
    psum x1 -> x0, waiting for transfers between devices: 102 us -> none  [local_step(): mixed_sum = lax.psum(partial, ('heads', 'model'))]
    pallas_call x0 -> x1, Pallas kernels: none -> 60.1 us  [local_step(): pl.pallas_call(functools.partial(step_kernel, dims), out_shape=(jax.Shape...]
    dot_general x7 -> x0, matrix products: 32 us -> none  [the longest x1 11.2 us: attend(): jnp.einsum('bgrd,bgtd->bgrt', queries, key_rows, preferred_element_type=j...]
    all_to_all x1 -> x0, blocking collectives: 9.47 us -> none  [local_step(): lax.all_to_all(attended.reshape(local_rows, heads_shard, head_dim), 'mode...]
    all_to_all x1 -> x0, starting transfers between devices: 6.02 us -> none  [local_step(): lax.all_to_all(queries.reshape(batch_all, heads_local, head_dim), 'model'...]
    unnamed x15 -> x3, local copies, waits for them, and re-layouts: 1.43 us -> 6.09 us
    convert_element_type x3 -> x0, other arithmetic: 4.13 us -> none  [the longest x1 4.07 us: local_step(): out_tokens = (tokens.astype(jnp.float32) + mixed_sum).astype(jnp.bfloat16)]
    reduce_sum x1 -> x0, other arithmetic: 1.76 us -> none  [attend(): denom_sum = jnp.sum(weights, axis=-1) + weight_new]
  transfers between devices with their start and end apart: 2 -> 0, of which waited for: 1 -> 0; matrix products, arithmetic and copies ran while one was open for 4% -> 0% of each run, Pallas kernels for 0% -> 0%
where the time goes in v1:
time: 67 us; the launch traced here: 66.8 us
  Pallas kernels  60.1 us (90%)
  local copies, waits for them, and re-layouts  6.09 us (9%)
    pallas_call x1, Pallas kernels, local_step(): pl.pallas_call(functools.partial(step_kernel, dims), out_shape=(jax.Shape...  60.1 us
    unnamed x3, local copies, waits for them, and re-layouts  6.09 us

profile of v1, /device:TPU:97, one launch (start us, length us, event | category | flops | bytes accessed | tf_op | source)
XLA Modules:
  0.0 66.8 jit_solution(17548579983055771693)
XLA Ops:
  0.6 60.1 %decode_step.1 = (bf16[4,2,32,4096]{3,2,1,0:T(8,128)(2,1)}, bf16[32,1024]{1,0:T(8,128)(2,1)}, bf16[32,1024]{1,0:T(8,128)(2,1)}) custom-call(bf16[4,2,32,4096]{3,2,1,0:T(8,128)(2,1)} %bitcast.6, bf16[4096,128]{1,0:T(8,128)(2,1)} %w_query.1, bf16[4096,1024]{1,0:T(8,128)(2,1)} %w_key.1, bf16[4096,1024]{1,0:T(8,128)(2,1)} %w_value.1, bf16[128,4096]{1,0:T(8,128)(2,1)} %w_out.1, ...), custom_call_target="tpu_custom_call" | custom-call | tf_op jit(solution)/shard_map/decode_step/pallas_call | solution.py:350
  60.7 1.5 %copy.11 = bf16[4,8,8,128]{3,2,1,0:T(8,128)(2,1)} copy(bf16[4,8,8,128]{3,1,2,0:T(8,128)(2,1)} %bitcast.11) | data formatting | bytes 131072
  62.2 1.5 %copy.12 = bf16[4,8,8,128]{3,2,1,0:T(8,128)(2,1)} copy(bf16[4,8,8,128]{3,1,2,0:T(8,128)(2,1)} %bitcast.10) | data formatting | bytes 131072
  63.7 3.1 %copy.14 = bf16[256,4096]{1,0:T(8,128)(2,1)} copy(bf16[256,4096]{1,0:T(8,128)(2,1)} %bitcast.7) | data formatting | bytes 4194304
